TPU v7x, 32 devices: a whole 2x2x4 slice. The times are simulated.
32 devices in a mesh: blk: 8 (over y, x, core), grp: 4 (over z).
Axes of the slice: x: 2, y: 2, z: 4, core: 2. Of those that a mesh axis runs over, the one named last changes fastest.
Arguments:
- queries: bfloat16 [8192, 4096], P(('blk', 'grp')), may hold values from -1 to 1
- documents: bfloat16 [8192, 4096], P(('blk', 'grp')), may hold values from -1 to 1
- positives: int32 [32, 256], P(('blk', 'grp')), may hold values from 0 to 255, as said below
Outputs:
- query_grad: float32 [8192, 4096], P(('blk', 'grp'))
- doc_grad: float32 [8192, 4096], P(('blk', 'grp'))
- loss: float32 [], replicated
Inputs may be any that keep to these rules, and one draw needn't show every extreme that they name: `positives`: each block of 256 rows names each of 0 to 255 exactly once.
All inputs are finite; a program needn't handle non-finite values.
Results may differ from a plain program's by a relative error of at most 0.0036.
Values may be sent and summed in bfloat16 or wider, within the bound.
A program may use at most 128 MiB of HBM per device.

v0:
```python
import functools

import jax
import jax.numpy as jnp
from jax import lax
from jax.experimental import pallas as pl
from jax.experimental.pallas import tpu as pltpu
from jax.sharding import PartitionSpec as P

SCALE = 50.0
EPSILON = 1e-06


def from_behind(value, axis, steps):
    count = lax.axis_size(axis)
    pairs = [(source, (source + steps) % count) for source in range(count)]
    return lax.ppermute(value, axis, pairs)


def normalize(raw):
    wide = raw.astype(jnp.float32)
    ratio = lax.rsqrt(jnp.sum(wide * wide, axis=-1, keepdims=True) + EPSILON)
    return ((wide * ratio).astype(jnp.bfloat16), wide, ratio)


def pull_back(grad, wide, ratio):
    inner = jnp.sum(wide * grad, axis=-1, keepdims=True)
    return ratio * grad - ratio * ratio * ratio * inner * wide


def score_block(left, right):
    return SCALE * jnp.einsum("id,jd->ij", left, right, preferred_element_type=jnp.float32)


def transpose_product(weights, left):
    return SCALE * jnp.einsum("ij,id->jd", weights, left, preferred_element_type=jnp.float32)


def on_device_plain(queries, documents, positives):
    norm_q, wide_q, ratio_q = normalize(queries)
    norm_d, wide_d, ratio_d = normalize(documents)
    width = lax.axis_size("blk")
    far = width // 4
    offsets = [1, -1, far, -far]
    rows = norm_q.shape[0]
    received = [norm_d]
    for off in offsets:
        received.append(from_behind(norm_d, "blk", off))
    scores = [score_block(norm_q, block) for block in received]
    total = scores[0].shape[0] * 0.0 + jnp.zeros((rows,), jnp.float32)
    for block_scores in scores:
        total = total + jnp.sum(jnp.exp(block_scores), axis=-1)
    lse = jnp.log(total)
    columns = jnp.arange(rows, dtype=jnp.int32)
    hot = (columns[None, :] == positives[0][:, None]).astype(jnp.float32)
    spos = jnp.sum(scores[0] * hot, axis=-1)
    part = jnp.sum(lse - spos)
    weights = [(jnp.exp(scores[0] - lse[:, None]) - hot).astype(jnp.bfloat16)]
    for block_scores in scores[1:]:
        weights.append(jnp.exp(block_scores - lse[:, None]).astype(jnp.bfloat16))
    query_dir = jnp.zeros_like(wide_q)
    for weight, block in zip(weights, received):
        query_dir = query_dir + SCALE * jnp.dot(weight, block, preferred_element_type=jnp.float32)
    doc_dir = transpose_product(weights[0], norm_q)
    for off, weight in zip(offsets, weights[1:]):
        partial_grad = transpose_product(weight, norm_q)
        doc_dir = doc_dir + from_behind(partial_grad.astype(jnp.bfloat16), "blk", -off).astype(
            partial_grad.dtype
        )
    query_grad = pull_back(query_dir, wide_q, ratio_q)
    doc_grad = pull_back(doc_dir, wide_d, ratio_d)
    summed = lax.psum(part, ("blk", "grp"))
    loss = summed / (rows * width * lax.axis_size("grp"))
    return (query_grad, doc_grad, loss)

CORES = 2
MESH = pl.DeviceIdType.MESH
CHUNK = 32
AHEAD = 3
TILE = 512
DEEP = 1024
NEAR, DIAG, RELAY, SIBLING = range(4)


def columns(n, size):
    return pl.ds(pl.multiple_of(n * size, size), size)


def wide_dot(left, right, contract):
    return lax.dot_general(left, right, ((contract[:1], contract[1:]), ((), ())), preferred_element_type=jnp.float32)


def kernel(
    n_blk, n_grp,
    queries, documents, positives,
    query_grad, doc_grad, loss,
    own, got, norm_d, norm_q, group_q, scores, weights, turned, ratio_q, ratio_d, inner,
    lse_own, lse_got, lse_wide, sums, sums_got,
    load_sem, x_send, x_recv, y_send, y_recv, r_send, r_recv, s_send, s_recv, l_send, l_recv, t_send, t_recv,
):
    rows, width = queries.shape
    per = rows // CHUNK
    chunks = 2 * per
    me, grp = lax.axis_index("blk"), lax.axis_index("grp")
    core, x, y = me % 2, (me // 2) % 2, me // 4
    sibling = me + 1 - 2 * core
    near = me + 2 - 4 * x
    across = me + 4 - 8 * y
    diag = near + 4 - 8 * y
    relay = lax.rem(me + n_blk - 1 + 2 * core, n_blk)
    relay_from = lax.rem(x + core, 2)
    grp_bits = [1 << n for n in range(n_grp.bit_length() - 1)]
    peers = [(sibling, grp), (near, grp), (across, grp)]
    for bit in grp_bits:
        peers.append((me, grp + bit - 2 * bit * ((grp // bit) % 2)))

    def remote(source, target, send, recv, device):
        return pltpu.make_async_remote_copy(
            src_ref=source, dst_ref=target, send_sem=send, recv_sem=recv, device_id=device, device_id_type=MESH
        )

    def piece(n):
        return pl.ds(pl.multiple_of(n * CHUNK, CHUNK), CHUNK)

    def x_copy(n):
        return remote(own.at[piece(n)], got.at[NEAR, piece(n)], x_send.at[n], x_recv.at[n], (near, grp))

    def y_copy(n):
        return remote(got.at[NEAR, piece(n)], got.at[DIAG, piece(n)], y_send.at[n], y_recv.at[n], (across, grp))

    def r_copy(n):
        return remote(
            got.at[relay_from, piece(n)], got.at[RELAY, piece(n)], r_send.at[n], r_recv.at[n], (sibling, grp)
        )

    def s_copy(half):
        cut = pl.ds(half * rows, rows)
        return remote(own.at[cut], got.at[SIBLING, cut], s_send.at[half], s_recv.at[half], (sibling, grp))

    lse_peers = [near, diag, relay, sibling]

    def lse_copy(n):
        return remote(lse_own, lse_got.at[n], l_send.at[n], l_recv.at[n], (lse_peers[n], grp))

    def sum_copy(n):
        return remote(sums.at[n], sums_got.at[n], t_send.at[n], t_recv.at[n], peers[n])

    load_d = pltpu.make_async_copy(documents, own.at[pl.ds(0, rows)], load_sem.at[0])
    load_q = pltpu.make_async_copy(queries, own.at[pl.ds(rows, rows)], load_sem.at[1])
    load_d.start()
    load_q.start()
    barrier = pltpu.get_barrier_semaphore()
    greeted = peers + [(diag, grp), (relay, grp)]
    for device in greeted:
        pl.semaphore_signal(barrier, inc=1, device_id=device, device_id_type=MESH)
    pl.semaphore_wait(barrier, len(greeted))
    load_d.wait()
    for n in range(AHEAD):
        x_copy(n).start()
    s_copy(0).start()
    load_q.wait()

    def normalized(raw):
        wide = raw.astype(jnp.float32)
        ratio = lax.rsqrt(jnp.sum(wide * wide, axis=-1, keepdims=True) + EPSILON)
        return (wide * ratio).astype(jnp.bfloat16), ratio

    def normalize_own(n, _):
        cut = piece(n)
        norm_d[cut, :], ratio_d[cut, :] = normalized(own[cut, :])
        norm_q[cut, :], ratio_q[cut, :] = normalized(own[piece(n + per), :])
        return 0

    def score(left, right, right_rows, target):
        def body(n, _):
            cut = columns(n, DEEP)
            term = SCALE * wide_dot(left[:, cut], right[right_rows, cut], (1, 1))

            @pl.when(n == 0)
            def _():
                target[...] = term

            @pl.when(n > 0)
            def _():
                target[...] += term
            return 0

        lax.fori_loop(0, width // DEEP, body, 0)

    def transposed(value):
        return jnp.transpose(value)

    def add_doc_terms(left, first):
        def body(n, _):
            cut = columns(n, TILE)
            term = SCALE * wide_dot(turned[...], left[:, cut], (1, 0))
            doc_grad[:, cut] = term if first else doc_grad[:, cut] + term
            return 0

        lax.fori_loop(0, width // TILE, body, 0)

    def pull_back_into(grad, raw_rows, ratio_ref):
        inner[...] = jnp.zeros_like(inner)

        def gather(n, _):
            cut = columns(n, TILE)
            prod = own[raw_rows, cut].astype(jnp.float32) * grad[:, cut]
            total = prod[:, :128]
            for k in range(1, TILE // 128):
                total = total + prod[:, k * 128 : (k + 1) * 128]
            inner[...] += total
            return 0

        lax.fori_loop(0, width // TILE, gather, 0)
        ratio = ratio_ref[...]
        factor = ratio * ratio * ratio * jnp.sum(inner[...], axis=-1, keepdims=True)

        def spread(n, _):
            cut = columns(n, TILE)
            grad[:, cut] = ratio * grad[:, cut] - factor * own[raw_rows, cut].astype(jnp.float32)
            return 0

        lax.fori_loop(0, width // TILE, spread, 0)

    def pump(n):
        if n < chunks:
            x_copy(n).wait_recv()
            y_copy(n).start()
            if n + AHEAD < chunks:
                x_copy(n + AHEAD).start()
        if 0 <= n - 2 < chunks:
            y_copy(n - 2).wait_recv()
            r_copy(n - 2).start()
        if 0 <= n - 3 < chunks:
            r_copy(n - 3).wait_recv()

    def normalize_documents(n):
        for k in (NEAR, DIAG, RELAY):
            norm_d[pl.ds((2 + k) * rows + n * CHUNK, CHUNK), :] = normalized(got[k, pl.ds(n * CHUNK, CHUNK), :])[0]

    def normalize_group(n):
        step = rows // 4
        for k in (NEAR, DIAG, RELAY, SIBLING):
            def body(m, _, k=k):
                value = got[k, pl.ds(pl.multiple_of(rows + n * step + m * 16, 16), 16), :]
                group_q[pl.ds(pl.multiple_of(k * step + m * 16, 16), 16), :] = normalized(value)[0]
                return 0
            lax.fori_loop(0, step // 16, body, 0)

    def add_group(n):
        step = rows // 4
        score(group_q, norm_d, pl.ds(0, rows), scores.at[:, pl.ds(0, rows)])
        lse = jnp.concatenate([lse_wide[k, n * step : (n + 1) * step, :] for k in range(4)], axis=0)[:, :1]
        turned[...] = transposed(jnp.exp(scores[:, :rows] - lse)).astype(jnp.bfloat16)
        add_doc_terms(group_q, False)

    lax.fori_loop(0, per, normalize_own, 0)
    s_copy(1).start()
    score(norm_q, norm_d, pl.ds(0, rows), scores.at[:, pl.ds(0, rows)])
    pump(0)
    s_copy(0).wait_recv()

    def normalize_sibling(n, _):
        cut = pl.ds(pl.multiple_of(rows + n * CHUNK, CHUNK), CHUNK)
        norm_d[cut, :] = normalized(got[SIBLING, piece(n), :])[0]
        return 0

    lax.fori_loop(0, per, normalize_sibling, 0)
    score(norm_q, norm_d, pl.ds(rows, rows), scores.at[:, pl.ds(rows, rows)])
    for n in range(1, per + 3):
        pump(n)
        if n >= 3:
            normalize_documents(n - 3)
    score(norm_q, norm_d, pl.ds(2 * rows, 3 * rows), scores.at[:, pl.ds(2 * rows, 3 * rows)])
    total = jnp.zeros((rows, 1), jnp.float32)
    for k in range(5):
        total = total + jnp.sum(jnp.exp(scores[:, k * rows : (k + 1) * rows]), axis=-1, keepdims=True)
    lse = jnp.log(total)
    lse_own[...] = transposed(jnp.broadcast_to(lse, (rows, 128)))[:8, :]
    named = jnp.broadcast_to(positives[...].astype(jnp.float32), (rows, rows))
    place = lax.broadcasted_iota(jnp.int32, (rows, rows), 0).astype(jnp.float32)
    hot = transposed((place == named).astype(jnp.float32))
    for k in range(5):
        value = jnp.exp(scores[:, k * rows : (k + 1) * rows] - lse)
        if k == 0:
            value = value - hot
            turned[...] = transposed(value).astype(jnp.bfloat16)
        weights[:, k * rows : (k + 1) * rows] = value.astype(jnp.bfloat16)
    part = jnp.sum(lse) - jnp.sum(scores[:, :rows] * hot)
    sums[0] = jnp.full((8, 128), part, jnp.float32)
    pump(per + 3)
    for k in range(4):
        lse_copy(k).start()
    sum_copy(0).start()

    def query_terms(n, _):
        cut = columns(n, TILE)
        query_grad[:, cut] = SCALE * wide_dot(weights[...], norm_d[:, cut], (1, 0))
        return 0

    lax.fori_loop(0, width // TILE, query_terms, 0)
    pump(per + 4)
    pull_back_into(query_grad, pl.ds(rows, rows), ratio_q)
    add_doc_terms(norm_q, True)
    s_copy(1).wait_recv()
    for k in range(4):
        lse_copy(k).wait_recv()
        value = jnp.broadcast_to(lse_got[k, :1, :], (128, rows))
        lse_wide[k] = transposed(value)
    done = 0
    rounds = 0

    def next_round(rounds):
        sum_copy(rounds).wait_recv()
        sums[rounds + 1] = sums[rounds] + sums_got[rounds]

    for n in range(per + 5, chunks + 3):
        pump(n)
        if rounds < len(peers):
            next_round(rounds)
            rounds += 1
        ready = (n - 3 - per + 1) * 4 // per
        while done < ready:
            normalize_group(done)
            add_group(done)
            done += 1
        if 0 < rounds < len(peers):
            sum_copy(rounds).start()
    while rounds < len(peers):
        next_round(rounds)
        rounds += 1
        if rounds < len(peers):
            sum_copy(rounds).start()
    pull_back_into(doc_grad, pl.ds(0, rows), ratio_d)
    loss[0, 0] = jnp.max(sums[len(peers)]) / (rows * n_blk * n_grp)

    def drain(n, _):
        x_copy(n).wait_send()
        y_copy(n).wait_send()
        r_copy(n).wait_send()
        return 0

    lax.fori_loop(0, chunks, drain, 0)
    for half in range(2):
        s_copy(half).wait_send()
    for k in range(4):
        lse_copy(k).wait_send()
    for k in range(len(peers)):
        sum_copy(k).wait_send()


def on_device_relay(queries, documents, positives):
    n_blk, n_grp = lax.axis_size("blk"), lax.axis_size("grp")
    rows, width = queries.shape
    chunks = 2 * rows // CHUNK
    rounds = 3 + n_grp.bit_length() - 1
    narrow, wide = jnp.bfloat16, jnp.float32
    dma = pltpu.SemaphoreType.DMA
    grad = pltpu.VMEM((rows, width), wide)
    query_grad, doc_grad, loss = pl.pallas_call(
        functools.partial(kernel, n_blk, n_grp),
        out_shape=[grad, grad, jax.ShapeDtypeStruct((1, 1), wide)],
        in_specs=[
            pl.BlockSpec(memory_space=pl.ANY),
            pl.BlockSpec(memory_space=pl.ANY),
            pl.BlockSpec(memory_space=pltpu.VMEM),
        ],
        out_specs=[
            pl.BlockSpec(memory_space=pltpu.VMEM),
            pl.BlockSpec(memory_space=pltpu.VMEM),
            pl.BlockSpec(memory_space=pltpu.SMEM),
        ],
        scratch_shapes=[
            pltpu.VMEM((2 * rows, width), narrow),
            pltpu.VMEM((4, 2 * rows, width), narrow),
            pltpu.VMEM((5 * rows, width), narrow),
            pltpu.VMEM((rows, width), narrow),
            pltpu.VMEM((rows, width), narrow),
            pltpu.VMEM((rows, 5 * rows), wide),
            pltpu.VMEM((rows, 5 * rows), narrow),
            pltpu.VMEM((rows, rows), narrow),
            pltpu.VMEM((rows, 1), wide),
            pltpu.VMEM((rows, 1), wide),
            pltpu.VMEM((rows, 128), wide),
            pltpu.VMEM((8, rows), wide),
            pltpu.VMEM((4, 8, rows), wide),
            pltpu.VMEM((4, rows, 128), wide),
            pltpu.VMEM((rounds + 1, 8, 128), wide),
            pltpu.VMEM((rounds, 8, 128), wide),
            dma((2,)),
            dma((chunks,)), dma((chunks,)), dma((chunks,)), dma((chunks,)), dma((chunks,)), dma((chunks,)),
            dma((2,)), dma((2,)), dma((4,)), dma((4,)), dma((rounds,)), dma((rounds,)),
        ],
        compiler_params=pltpu.CompilerParams(
            collective_id=0, has_side_effects=True, vmem_limit_bytes=52 * 1024 * 1024
        ),
    )(queries, documents, positives)
    return query_grad, doc_grad, loss.reshape(())


def fits(n_blk, n_grp):
    return n_blk == 4 * CORES and n_grp & (n_grp - 1) == 0


def on_device(queries, documents, positives):
    if fits(lax.axis_size("blk"), lax.axis_size("grp")):
        return on_device_relay(queries, documents, positives)
    return on_device_plain(queries, documents, positives)


def solution(mesh):
    return jax.shard_map(
        on_device,
        mesh=mesh,
        in_specs=(P(("blk", "grp"), None), P(("blk", "grp"), None), P(("blk", "grp"), None)),
        out_specs=(P(("blk", "grp"), None), P(("blk", "grp"), None), P()),
        check_vma=False,
    )
```

profile of v0, /device:TPU:0, one launch (start us, length us, event | category | flops | bytes accessed | tf_op | source)
XLA Modules:
  0.0 138.1 jit_solution(11605398325822125637)
XLA Ops:
  0.6 131.8 %shard_map.58 = (f32[256,4096]{1,0:T(8,128)S(1)}, f32[256,4096]{1,0:T(8,128)S(1)}, f32[1,1]{1,0:T(1,128)}) custom-call(bf16[256,4096]{1,0:T(8,128)(2,1)} %queries.1, bf16[256,4096]{1,0:T(8,128)(2,1)} %documents.1, s32[1,256]{1,0:T(1,128)} %positives.1), custom_call_target="tpu_custom_call" | custom-call | tf_op jit(solution)/shard_map/pallas_call | solution.py:360
  132.4 2.0 %copy.9 = f32[256,4096]{1,0:T(8,128)} copy(f32[256,4096]{1,0:T(8,128)S(1)} %get-tuple-element.9) | data formatting | bytes 8388608
  134.4 2.0 %copy.10 = f32[256,4096]{1,0:T(8,128)} copy(f32[256,4096]{1,0:T(8,128)S(1)} %get-tuple-element.10) | data formatting | bytes 8388608
where the time goes:
time: 138 us
  Pallas kernels  132 us (96%)
  local copies, waits for them, and re-layouts  4.03 us (3%)
  between operations  2.33 us (2%)
    pallas_call x1, Pallas kernels, on_device_relay(): pl.pallas_call(functools.partial(kernel, n_blk, n_grp), out_shape=[grad,...  132 us
    unnamed x2, local copies, waits for them, and re-layouts  4.03 us

commit v1 on v0

v1 whole, which is shorter than its diff:
```python
import functools

import jax
import jax.numpy as jnp
from jax import lax
from jax.experimental import pallas as pl
from jax.experimental.pallas import tpu as pltpu
from jax.sharding import PartitionSpec as P

SCALE = 50.0
EPSILON = 1e-06


def from_behind(value, axis, steps):
    count = lax.axis_size(axis)
    pairs = [(source, (source + steps) % count) for source in range(count)]
    return lax.ppermute(value, axis, pairs)


def normalize(raw):
    wide = raw.astype(jnp.float32)
    ratio = lax.rsqrt(jnp.sum(wide * wide, axis=-1, keepdims=True) + EPSILON)
    return ((wide * ratio).astype(jnp.bfloat16), wide, ratio)


def pull_back(grad, wide, ratio):
    inner = jnp.sum(wide * grad, axis=-1, keepdims=True)
    return ratio * grad - ratio * ratio * ratio * inner * wide


def score_block(left, right):
    return SCALE * jnp.einsum("id,jd->ij", left, right, preferred_element_type=jnp.float32)


def transpose_product(weights, left):
    return SCALE * jnp.einsum("ij,id->jd", weights, left, preferred_element_type=jnp.float32)


def on_device_plain(queries, documents, positives):
    norm_q, wide_q, ratio_q = normalize(queries)
    norm_d, wide_d, ratio_d = normalize(documents)
    width = lax.axis_size("blk")
    far = width // 4
    offsets = [1, -1, far, -far]
    rows = norm_q.shape[0]
    received = [norm_d]
    for off in offsets:
        received.append(from_behind(norm_d, "blk", off))
    scores = [score_block(norm_q, block) for block in received]
    total = scores[0].shape[0] * 0.0 + jnp.zeros((rows,), jnp.float32)
    for block_scores in scores:
        total = total + jnp.sum(jnp.exp(block_scores), axis=-1)
    lse = jnp.log(total)
    columns = jnp.arange(rows, dtype=jnp.int32)
    hot = (columns[None, :] == positives[0][:, None]).astype(jnp.float32)
    spos = jnp.sum(scores[0] * hot, axis=-1)
    part = jnp.sum(lse - spos)
    weights = [(jnp.exp(scores[0] - lse[:, None]) - hot).astype(jnp.bfloat16)]
    for block_scores in scores[1:]:
        weights.append(jnp.exp(block_scores - lse[:, None]).astype(jnp.bfloat16))
    query_dir = jnp.zeros_like(wide_q)
    for weight, block in zip(weights, received):
        query_dir = query_dir + SCALE * jnp.dot(weight, block, preferred_element_type=jnp.float32)
    doc_dir = transpose_product(weights[0], norm_q)
    for off, weight in zip(offsets, weights[1:]):
        partial_grad = transpose_product(weight, norm_q)
        doc_dir = doc_dir + from_behind(partial_grad.astype(jnp.bfloat16), "blk", -off).astype(
            partial_grad.dtype
        )
    query_grad = pull_back(query_dir, wide_q, ratio_q)
    doc_grad = pull_back(doc_dir, wide_d, ratio_d)
    summed = lax.psum(part, ("blk", "grp"))
    loss = summed / (rows * width * lax.axis_size("grp"))
    return (query_grad, doc_grad, loss)

CORES = 2
MESH = pl.DeviceIdType.MESH
CHUNK = 16
SPLIT = 1
PARTS = 8
LAG = 2
BUDGET = 3.5
GROUPS = (10, 4, 2)
AHEAD = 2
TILE = 512
DEEP = 1024
NEAR, DIAG, RELAY, SIBLING = range(4)


def columns(n, size):
    return pl.ds(pl.multiple_of(n * size, size), size)


def wide_dot(left, right, contract):
    return lax.dot_general(left, right, ((contract[:1], contract[1:]), ((), ())), preferred_element_type=jnp.float32)


def kernel(
    n_blk, n_grp,
    queries, documents, positives,
    query_grad, doc_grad, loss,
    own, got, norm_d, norm_q, sibling_q, group_q, scores, group_scores, weights, turned, ratio_q, ratio_d, inner,
    lse_own, lse_got, lse_wide, lse_group, sums, sums_got,
    load_sem, x_send, x_recv, y_send, y_recv, r_send, r_recv, s_send, s_recv, l_send, l_recv, t_send, t_recv,
):
    rows, width = queries.shape
    per = rows // CHUNK
    copies = 2 * per * SPLIT
    part_rows = 2 * rows // PARTS
    me, grp = lax.axis_index("blk"), lax.axis_index("grp")
    core, x, y = me % 2, (me // 2) % 2, me // 4
    sibling = me + 1 - 2 * core
    near = me + 2 - 4 * x
    across = me + 4 - 8 * y
    diag = near + 4 - 8 * y
    relay = lax.rem(me + n_blk - 1 + 2 * core, n_blk)
    relay_from = lax.rem(x + core, 2)
    peers = [(sibling, grp), (near, grp), (across, grp)]
    for bit in [1 << n for n in range(n_grp.bit_length() - 1)]:
        peers.append((me, grp + bit - 2 * bit * ((grp // bit) % 2)))

    def remote(source, target, send, recv, device):
        return pltpu.make_async_remote_copy(
            src_ref=source, dst_ref=target, send_sem=send, recv_sem=recv, device_id=device, device_id_type=MESH
        )

    def piece(n):
        size = width // SPLIT
        return (
            pl.ds(pl.multiple_of((n // SPLIT) * CHUNK, CHUNK), CHUNK),
            pl.ds(pl.multiple_of((n % SPLIT) * size, size), size),
        )

    def x_copy(n):
        r, c = piece(n)
        return remote(own.at[r, c], got.at[NEAR, r, c], x_send.at[n], x_recv.at[n], (near, grp))

    def y_copy(n):
        r, c = piece(n)
        return remote(got.at[NEAR, r, c], got.at[DIAG, r, c], y_send.at[n], y_recv.at[n], (across, grp))

    def r_copy(n):
        r, c = piece(n)
        return remote(got.at[relay_from, r, c], got.at[RELAY, r, c], r_send.at[n], r_recv.at[n], (sibling, grp))

    def s_copy(n):
        cut = pl.ds(n * part_rows, part_rows)
        return remote(own.at[cut], got.at[SIBLING, cut], s_send.at[n], s_recv.at[n], (sibling, grp))

    lse_peers = [near, diag, relay, sibling]

    def lse_copy(n):
        return remote(lse_own, lse_got.at[n], l_send.at[n], l_recv.at[n], (lse_peers[n], grp))

    def sum_copy(n):
        return remote(sums.at[n], sums_got.at[n], t_send.at[n], t_recv.at[n], peers[n])

    load_d = pltpu.make_async_copy(documents, own.at[pl.ds(0, rows)], load_sem.at[0])
    load_q = pltpu.make_async_copy(queries, own.at[pl.ds(rows, rows)], load_sem.at[1])
    load_d.start()
    load_q.start()
    group_scores[...] = jnp.zeros_like(group_scores)
    barrier = pltpu.get_barrier_semaphore()
    greeted = peers + [(diag, grp), (relay, grp)]
    for device in greeted:
        pl.semaphore_signal(barrier, inc=1, device_id=device, device_id_type=MESH)
    pl.semaphore_wait(barrier, len(greeted))
    load_d.wait()
    for n in range(AHEAD):
        x_copy(n).start()
    load_q.wait()

    def normalized(raw):
        wide = raw.astype(jnp.float32)
        ratio = lax.rsqrt(jnp.sum(wide * wide, axis=-1, keepdims=True) + EPSILON)
        return (wide * ratio).astype(jnp.bfloat16), ratio

    def at(start, size):
        return pl.ds(start, size)

    def normalize_own(first):
        for start in range(first, first + 32, 16):
            cut = at(start, 16)
            norm_d[cut, :], ratio_d[cut, :] = normalized(own[cut, :])
            norm_q[cut, :], ratio_q[cut, :] = normalized(own[at(rows + start, 16), :])

    def normalize_into(target, target_row, source, row, count):
        for start in range(0, count, 16):
            target[at(target_row + start, 16), :] = normalized(got[source, at(row + start, 16), :])[0]

    def score(left, left_rows, right, right_rows, target):
        def body(n, _):
            cut = columns(n, DEEP)
            term = SCALE * wide_dot(left[left_rows, cut], right[right_rows, cut], (1, 1))

            @pl.when(n == 0)
            def _():
                target[...] = term

            @pl.when(n > 0)
            def _():
                target[...] += term
            return 0

        lax.fori_loop(0, width // DEEP, body, 0)

    def loop(first, last, body):
        lax.fori_loop(first, last, lambda n, _: (body(n), 0)[1], 0)

    tiles = width // TILE

    def doc_terms(left, left_rows, depth, place, first, low, high):
        def body(n):
            cut = columns(n, TILE)
            term = SCALE * wide_dot(turned[:, place : place + depth], left[left_rows, cut], (1, 0))
            doc_grad[:, cut] = term if first else doc_grad[:, cut] + term

        loop(low, high, body)

    def gather(grad, raw_rows):
        inner[...] = jnp.zeros_like(inner)

        def body(n):
            cut = columns(n, TILE)
            prod = own[raw_rows, cut].astype(jnp.float32) * grad[:, cut]
            total = prod[:, :128]
            for k in range(1, TILE // 128):
                total = total + prod[:, k * 128 : (k + 1) * 128]
            inner[...] += total

        loop(0, tiles, body)

    def spread(grad, raw_rows, ratio_ref):
        ratio = ratio_ref[...]
        factor = ratio * ratio * ratio * jnp.sum(inner[...], axis=-1, keepdims=True)

        def body(n):
            cut = columns(n, TILE)
            grad[:, cut] = ratio * grad[:, cut] - factor * own[raw_rows, cut].astype(jnp.float32)

        loop(0, tiles, body)

    soon, later, state = [], [], {"now": 0, "lse": False}
    all_rows = at(0, rows)
    doc_rows, query_rows = at(0, rows), at(rows, rows)

    def block(k):
        return pl.ds(k * rows, rows)

    def put(ready, cost, step):
        later.append((ready, cost, step))

    def in_(delay, step):
        soon.append((state["now"] + delay, step))

    def send_sibling(n):
        s_copy(n).start()

    for n in range(PARTS):
        soon.append((n * SPLIT, functools.partial(send_sibling, n)))
    for first in range(0, rows, 32):
        put(0, 0.3, functools.partial(normalize_own, first))
    put(0, 1.2, lambda: score(norm_q, all_rows, norm_d, block(0), scores.at[:, block(0)]))

    def sibling_part(n):
        s_copy(n).wait_recv()
        row = n * part_rows
        if row < rows:
            normalize_into(norm_d, rows + row, SIBLING, row, part_rows)
        else:
            normalize_into(sibling_q, row - rows, SIBLING, row, part_rows)

    for n in range(PARTS):
        put((n + 2) * SPLIT, 0.3 * part_rows / 64, functools.partial(sibling_part, n))
        if (n + 1) * 2 == PARTS:
            put(0, 1.2, lambda: score(norm_q, all_rows, norm_d, block(1), scores.at[:, block(1)]))
    put(0, 1.2, lambda: score(sibling_q, all_rows, norm_d, block(0), scores.at[:, block(5)]))

    def arrived(n):
        if n < per:
            for k in (NEAR, DIAG, RELAY):
                normalize_into(norm_d, (2 + k) * rows + n * CHUNK, k, n * CHUNK, CHUNK)
        else:
            for k in (NEAR, DIAG, RELAY):
                normalize_into(group_q, ((n - per) * 3 + k) * CHUNK, k, n * CHUNK, CHUNK)

    for k in (2, 3, 4):
        put(per * SPLIT + 2, 1.2, functools.partial(
            lambda k: score(norm_q, all_rows, norm_d, block(k), scores.at[:, block(k)]), k))

    def log_sum():
        total = jnp.zeros((rows, 1), jnp.float32)
        for k in range(5):
            total = total + jnp.sum(jnp.exp(scores[:, k * rows : (k + 1) * rows]), axis=-1, keepdims=True)
        lse_wide[3] = jnp.broadcast_to(jnp.log(total), (rows, 128))
        lse_own[...] = jnp.transpose(lse_wide[3])[:8, :]
        in_(1, send_lse)

    def send_lse():
        for k in range(4):
            lse_copy(k).start()
        in_(2 * SPLIT, take_lse)

    def take_lse():
        for k in range(4):
            lse_copy(k).wait_recv()
            value = jnp.transpose(jnp.broadcast_to(lse_got[k, :1, :], (128, rows)))
            if k == SIBLING:
                lse_group[pl.ds(0, rows), :] = value
                continue
            for n in range(per):
                lse_group[pl.ds(rows + (n * 3 + k) * CHUNK, CHUNK), :] = value[n * CHUNK : (n + 1) * CHUNK, :]
        state["lse"] = True
        urgent.append((0, 0.3, sibling_weights))
        add_doc_steps(norm_q, all_rows, rows, 0, True)
        add_doc_steps(sibling_q, all_rows, rows, rows, False)

    def add_doc_steps(left, left_rows, depth, place, first, where=None):
        steps = 2 if SPLIT == 1 else 4
        for n in range(steps):
            urgent.append((0, 2.0 / steps, functools.partial(
                doc_terms, left, left_rows, depth, place, first, n * tiles // steps, (n + 1) * tiles // steps)))

    def sibling_weights():
        value = jnp.exp(scores[:, 5 * rows :] - lse_group[pl.ds(0, rows), :][:, :1])
        turned[:, rows : 2 * rows] = jnp.transpose(value).astype(jnp.bfloat16)

    def weight(k):
        value = jnp.exp(scores[:, k * rows : (k + 1) * rows] - lse_wide[3][:, :1])
        if k == 0:
            named = jnp.broadcast_to(positives[...].astype(jnp.float32), (rows, rows))
            place = lax.broadcasted_iota(jnp.int32, (rows, rows), 0).astype(jnp.float32)
            hot = jnp.transpose((place == named).astype(jnp.float32))
            value = value - hot
            turned[:, :rows] = jnp.transpose(value).astype(jnp.bfloat16)
            part = jnp.sum(lse_wide[3][:, :1]) - jnp.sum(scores[:, :rows] * hot)
            sums[0] = jnp.full((8, 128), part, jnp.float32)
            in_(1, functools.partial(send_sum, 0))
        weights[:, k * rows : (k + 1) * rows] = value.astype(jnp.bfloat16)

    def send_sum(n):
        sum_copy(n).start()
        in_(SPLIT, functools.partial(take_sum, n))

    def take_sum(n):
        sum_copy(n).wait_recv()
        sums[n + 1] = sums[n] + sums_got[n]
        if n + 1 < len(peers):
            in_(1, functools.partial(send_sum, n + 1))
        else:
            in_(1, give_loss)

    def give_loss():
        loss[0, 0] = jnp.max(sums[len(peers)]) / (rows * n_blk * n_grp)

    put(0, 1.0, log_sum)
    for k in range(5):
        put(0, 0.4 if k else 0.7, functools.partial(weight, k))

    def query_terms(low, high):
        def body(n):
            cut = columns(n, TILE)
            query_grad[:, cut] = SCALE * wide_dot(weights[...], norm_d[:, cut], (1, 0))

        loop(low, high, body)

    for n in range(0, tiles, 2):
        put(0, 1.0, functools.partial(query_terms, n, n + 2))
    put(0, 0.9, lambda: gather(query_grad, query_rows))
    put(0, 0.9, lambda: spread(query_grad, query_rows, ratio_q))
    urgent = []
    groups, start = [], 0
    for count in GROUPS:
        groups.append((start, count * per // 16))
        start += count * per // 16

    def group(index):
        start, count = groups[index]
        first, depth = start * 3 * CHUNK, count * 3 * CHUNK
        for low in range(0, depth, rows):
            size = min(rows, depth - low)
            urgent.append((0, 1.2, functools.partial(
                score, group_q, at(first + low, size), norm_d, block(0), group_scores.at[at(low, size), :])))

        def group_weights():
            value = jnp.exp(group_scores[at(0, depth), :] - lse_group[pl.ds(rows + first, depth), :][:, :1])
            group_scores[at(0, depth), :] = value
            turned[...] = jnp.transpose(group_scores[...]).astype(jnp.bfloat16)

        urgent.append((0, 0.5, group_weights))
        add_doc_steps(group_q, at(first, depth), depth, 0, False)

    waiting = [(per + start + count - 1, n) for n, (start, count) in enumerate(groups)]
    for n in range(copies + LAG + 1):
        state["now"] = n
        if n < copies:
            x_copy(n).wait_recv()
            y_copy(n).start()
            if n + AHEAD < copies:
                x_copy(n + AHEAD).start()
        m = n - LAG
        if 0 <= m < copies:
            y_copy(m).wait_recv()
            r_copy(m).start()
        m -= 1
        if 0 <= m < copies:
            r_copy(m).wait_recv()
        ready = [step for when, step in soon if when <= n]
        soon[:] = [(when, step) for when, step in soon if when > n]
        for step in ready:
            step()
        if m >= 0 and m % SPLIT == SPLIT - 1 and m < copies:
            arrived(m // SPLIT)
        while waiting and state["lse"] and waiting[0][0] * SPLIT + SPLIT - 1 <= m:
            group(waiting.pop(0)[1])
        spent = 0.0
        while urgent or (later and later[0][0] <= n):
            pool = urgent if urgent else later
            if spent and spent + pool[0][1] > BUDGET / SPLIT:
                break
            ready, cost, step = pool.pop(0)
            step()
            spent += cost
    while soon or urgent or later or waiting:
        state["now"] += 1
        while soon:
            soon.pop(0)[1]()
        while urgent:
            urgent.pop(0)[2]()
        if later:
            later.pop(0)[2]()
        elif waiting and state["lse"]:
            group(waiting.pop(0)[1])
    gather(doc_grad, doc_rows)
    spread(doc_grad, doc_rows, ratio_d)

    def drain(n, _):
        x_copy(n).wait_send()
        y_copy(n).wait_send()
        r_copy(n).wait_send()
        return 0

    lax.fori_loop(0, copies, drain, 0)
    for n in range(PARTS):
        s_copy(n).wait_send()
    for k in range(4):
        lse_copy(k).wait_send()
    for k in range(len(peers)):
        sum_copy(k).wait_send()


def on_device_relay(queries, documents, positives):
    n_blk, n_grp = lax.axis_size("blk"), lax.axis_size("grp")
    rows, width = queries.shape
    copies = 2 * rows // CHUNK * SPLIT
    rounds = 3 + n_grp.bit_length() - 1
    narrow, wide = jnp.bfloat16, jnp.float32
    dma = pltpu.SemaphoreType.DMA
    grad = pltpu.VMEM((rows, width), wide)
    query_grad, doc_grad, loss = pl.pallas_call(
        functools.partial(kernel, n_blk, n_grp),
        out_shape=[grad, grad, jax.ShapeDtypeStruct((1, 1), wide)],
        in_specs=[
            pl.BlockSpec(memory_space=pl.ANY),
            pl.BlockSpec(memory_space=pl.ANY),
            pl.BlockSpec(memory_space=pltpu.VMEM),
        ],
        out_specs=[
            pl.BlockSpec(memory_space=pltpu.VMEM),
            pl.BlockSpec(memory_space=pltpu.VMEM),
            pl.BlockSpec(memory_space=pltpu.SMEM),
        ],
        scratch_shapes=[
            pltpu.VMEM((2 * rows, width), narrow),
            pltpu.VMEM((4, 2 * rows, width), narrow),
            pltpu.VMEM((5 * rows, width), narrow),
            pltpu.VMEM((rows, width), narrow),
            pltpu.VMEM((rows, width), narrow),
            pltpu.VMEM((3 * rows, width), narrow),
            pltpu.VMEM((rows, 6 * rows), wide),
            pltpu.VMEM((2 * rows, rows), wide),
            pltpu.VMEM((rows, 5 * rows), narrow),
            pltpu.VMEM((rows, 2 * rows), narrow),
            pltpu.VMEM((rows, 1), wide),
            pltpu.VMEM((rows, 1), wide),
            pltpu.VMEM((rows, 128), wide),
            pltpu.VMEM((8, rows), wide),
            pltpu.VMEM((4, 8, rows), wide),
            pltpu.VMEM((4, rows, 128), wide),
            pltpu.VMEM((4 * rows, 128), wide),
            pltpu.VMEM((rounds + 1, 8, 128), wide),
            pltpu.VMEM((rounds, 8, 128), wide),
            dma((2,)),
            dma((copies,)), dma((copies,)), dma((copies,)), dma((copies,)), dma((copies,)), dma((copies,)),
            dma((PARTS,)), dma((PARTS,)), dma((4,)), dma((4,)), dma((rounds,)), dma((rounds,)),
        ],
        compiler_params=pltpu.CompilerParams(
            collective_id=0, has_side_effects=True, vmem_limit_bytes=55 * 1024 * 1024
        ),
    )(queries, documents, positives)
    return query_grad, doc_grad, loss.reshape(())


def fits(n_blk, n_grp):
    return n_blk == 4 * CORES and n_grp & (n_grp - 1) == 0


def on_device(queries, documents, positives):
    if fits(lax.axis_size("blk"), lax.axis_size("grp")):
        return on_device_relay(queries, documents, positives)
    return on_device_plain(queries, documents, positives)


def solution(mesh):
    return jax.shard_map(
        on_device,
        mesh=mesh,
        in_specs=(P(("blk", "grp"), None), P(("blk", "grp"), None), P(("blk", "grp"), None)),
        out_specs=(P(("blk", "grp"), None), P(("blk", "grp"), None), P()),
        check_vma=False,
    )
```

time: 138 us -> 121 us (0.88)
  Pallas kernels: 132 us -> 115 us
    pallas_call x1, Pallas kernels: 132 us -> 115 us  [on_device_relay(): pl.pallas_call(functools.partial(kernel, n_blk, n_grp), out_shape=[grad,...]
where the time goes in v1:
time: 121 us
  Pallas kernels  115 us (95%)
  local copies, waits for them, and re-layouts  4.03 us (3%)
  between operations  2.33 us (2%)
    pallas_call x1, Pallas kernels, on_device_relay(): pl.pallas_call(functools.partial(kernel, n_blk, n_grp), out_shape=[grad,...  115 us
    unnamed x2, local copies, waits for them, and re-layouts  4.03 us

profile of v1, /device:TPU:0, one launch (start us, length us, event | category | flops | bytes accessed | tf_op | source)
XLA Modules:
  0.0 121.0 jit_solution(14281618926987712417)
XLA Ops:
  0.6 114.7 %shard_map.58 = (f32[256,4096]{1,0:T(8,128)S(1)}, f32[256,4096]{1,0:T(8,128)S(1)}, f32[1,1]{1,0:T(1,128)}) custom-call(bf16[256,4096]{1,0:T(8,128)(2,1)} %queries.1, bf16[256,4096]{1,0:T(8,128)(2,1)} %documents.1, s32[1,256]{1,0:T(1,128)} %positives.1), custom_call_target="tpu_custom_call" | custom-call | tf_op jit(solution)/shard_map/pallas_call | solution.py:460
  115.3 2.0 %copy.9 = f32[256,4096]{1,0:T(8,128)} copy(f32[256,4096]{1,0:T(8,128)S(1)} %get-tuple-element.9) | data formatting | bytes 8388608
  117.3 2.0 %copy.10 = f32[256,4096]{1,0:T(8,128)} copy(f32[256,4096]{1,0:T(8,128)S(1)} %get-tuple-element.10) | data formatting | bytes 8388608

commit v2 on v1

--- a/solution.py
+++ b/solution.py
@@ -98,8 +98,8 @@
 def kernel(
     n_blk, n_grp,
     queries, documents, positives,
-    query_grad, doc_grad, loss,
-    own, got, norm_d, norm_q, sibling_q, group_q, scores, group_scores, weights, turned, ratio_q, ratio_d, inner,
+    query_grad, doc_grad, own, coefs, loss,
+    got, norm_d, norm_q, sibling_q, group_q, scores, group_scores, weights, turned, ratio_q, ratio_d, inner,
     lse_own, lse_got, lse_wide, lse_group, sums, sums_got,
     load_sem, x_send, x_recv, y_send, y_recv, r_send, r_recv, s_send, s_recv, l_send, l_recv, t_send, t_recv,
 ):
@@ -160,6 +160,7 @@
     load_d.start()
     load_q.start()
     group_scores[...] = jnp.zeros_like(group_scores)
+    inner[1] = jnp.zeros((rows, 128), jnp.float32)
     barrier = pltpu.get_barrier_semaphore()
     greeted = peers + [(diag, grp), (relay, grp)]
     for device in greeted:
@@ -209,30 +210,27 @@
 
     tiles = width // TILE
 
-    def doc_terms(left, left_rows, depth, place, first, low, high):
+    def doc_terms(left, left_rows, depth, place, first, last, low, high):
         def body(n):
             cut = columns(n, TILE)
             term = SCALE * wide_dot(turned[:, place : place + depth], left[left_rows, cut], (1, 0))
-            doc_grad[:, cut] = term if first else doc_grad[:, cut] + term
+            value = term if first else doc_grad[:, cut] + term
+            doc_grad[:, cut] = value
+            if last:
+                inner[1] += folded(own[doc_rows, cut].astype(jnp.float32) * value)
 
         loop(low, high, body)
 
-    def gather(grad, raw_rows):
-        inner[...] = jnp.zeros_like(inner)
-
-        def body(n):
-            cut = columns(n, TILE)
-            prod = own[raw_rows, cut].astype(jnp.float32) * grad[:, cut]
-            total = prod[:, :128]
-            for k in range(1, TILE // 128):
-                total = total + prod[:, k * 128 : (k + 1) * 128]
-            inner[...] += total
-
-        loop(0, tiles, body)
+    def folded(value):
+        total = value[:, :128]
+        for k in range(1, TILE // 128):
+            total = total + value[:, k * 128 : (k + 1) * 128]
+        return total
+
 
     def spread(grad, raw_rows, ratio_ref):
         ratio = ratio_ref[...]
-        factor = ratio * ratio * ratio * jnp.sum(inner[...], axis=-1, keepdims=True)
+        factor = ratio * ratio * ratio * jnp.sum(inner[0], axis=-1, keepdims=True)
 
         def body(n):
             cut = columns(n, TILE)
@@ -315,11 +313,11 @@
         add_doc_steps(norm_q, all_rows, rows, 0, True)
         add_doc_steps(sibling_q, all_rows, rows, rows, False)
 
-    def add_doc_steps(left, left_rows, depth, place, first, where=None):
+    def add_doc_steps(left, left_rows, depth, place, first, last=False):
         steps = 2 if SPLIT == 1 else 4
         for n in range(steps):
             urgent.append((0, 2.0 / steps, functools.partial(
-                doc_terms, left, left_rows, depth, place, first, n * tiles // steps, (n + 1) * tiles // steps)))
+                doc_terms, left, left_rows, depth, place, first, last, n * tiles // steps, (n + 1) * tiles // steps)))
 
     def sibling_weights():
         value = jnp.exp(scores[:, 5 * rows :] - lse_group[pl.ds(0, rows), :][:, :1])
@@ -360,13 +358,16 @@
     def query_terms(low, high):
         def body(n):
             cut = columns(n, TILE)
-            query_grad[:, cut] = SCALE * wide_dot(weights[...], norm_d[:, cut], (1, 0))
-
+            value = SCALE * wide_dot(weights[...], norm_d[:, cut], (1, 0))
+            query_grad[:, cut] = value
+            inner[0] += folded(own[query_rows, cut].astype(jnp.float32) * value)
+
+        if low == 0:
+            inner[0] = jnp.zeros((rows, 128), jnp.float32)
         loop(low, high, body)
 
     for n in range(0, tiles, 2):
         put(0, 1.0, functools.partial(query_terms, n, n + 2))
-    put(0, 0.9, lambda: gather(query_grad, query_rows))
     put(0, 0.9, lambda: spread(query_grad, query_rows, ratio_q))
     urgent = []
     groups, start = [], 0
@@ -388,7 +389,7 @@
             turned[...] = jnp.transpose(group_scores[...]).astype(jnp.bfloat16)
 
         urgent.append((0, 0.5, group_weights))
-        add_doc_steps(group_q, at(first, depth), depth, 0, False)
+        add_doc_steps(group_q, at(first, depth), depth, 0, False, index == len(groups) - 1)
 
     waiting = [(per + start + count - 1, n) for n, (start, count) in enumerate(groups)]
     for n in range(copies + LAG + 1):
@@ -431,8 +432,11 @@
             later.pop(0)[2]()
         elif waiting and state["lse"]:
             group(waiting.pop(0)[1])
-    gather(doc_grad, doc_rows)
-    spread(doc_grad, doc_rows, ratio_d)
+    ratio = ratio_d[...]
+    coefs[0] = jnp.broadcast_to(ratio, (rows, 128))
+    coefs[1] = jnp.broadcast_to(
+        ratio * ratio * ratio * jnp.sum(inner[1], axis=-1, keepdims=True), (rows, 128)
+    )
 
     def drain(n, _):
         x_copy(n).wait_send()
@@ -447,6 +451,21 @@
         lse_copy(k).wait_send()
     for k in range(len(peers)):
         sum_copy(k).wait_send()
+
+
+def finish(query_grad, doc_dir, own, coefs, query_out, doc_out, staged, sem):
+    rows = query_grad.shape[0]
+    step = rows // 8
+    copies = [pltpu.make_async_copy(query_grad, query_out, sem.at[8])]
+    copies[0].start()
+    for n in range(8):
+        cut = pl.ds(n * step, step)
+        ratio, factor = coefs[0, cut, :][:, :1], coefs[1, cut, :][:, :1]
+        staged[cut, :] = ratio * doc_dir[cut, :] - factor * own[cut, :].astype(jnp.float32)
+        copies.append(pltpu.make_async_copy(staged.at[cut], doc_out.at[cut], sem.at[n]))
+        copies[-1].start()
+    for copy in copies:
+        copy.wait()
 
 
 def on_device_relay(queries, documents, positives):
@@ -457,21 +476,20 @@
     narrow, wide = jnp.bfloat16, jnp.float32
     dma = pltpu.SemaphoreType.DMA
     grad = pltpu.VMEM((rows, width), wide)
-    query_grad, doc_grad, loss = pl.pallas_call(
+    vmem = pl.BlockSpec(memory_space=pltpu.VMEM)
+    anywhere = pl.BlockSpec(memory_space=pl.ANY)
+    query_grad, doc_dir, own, coefs, loss = pl.pallas_call(
         functools.partial(kernel, n_blk, n_grp),
-        out_shape=[grad, grad, jax.ShapeDtypeStruct((1, 1), wide)],
-        in_specs=[
-            pl.BlockSpec(memory_space=pl.ANY),
-            pl.BlockSpec(memory_space=pl.ANY),
-            pl.BlockSpec(memory_space=pltpu.VMEM),
+        out_shape=[
+            grad,
+            grad,
+            pltpu.VMEM((2 * rows, width), narrow),
+            pltpu.VMEM((2, rows, 128), wide),
+            jax.ShapeDtypeStruct((1, 1), wide),
         ],
-        out_specs=[
-            pl.BlockSpec(memory_space=pltpu.VMEM),
-            pl.BlockSpec(memory_space=pltpu.VMEM),
-            pl.BlockSpec(memory_space=pltpu.SMEM),
-        ],
+        in_specs=[anywhere, anywhere, vmem],
+        out_specs=[vmem, vmem, vmem, vmem, pl.BlockSpec(memory_space=pltpu.SMEM)],
         scratch_shapes=[
-            pltpu.VMEM((2 * rows, width), narrow),
             pltpu.VMEM((4, 2 * rows, width), narrow),
             pltpu.VMEM((5 * rows, width), narrow),
             pltpu.VMEM((rows, width), narrow),
@@ -483,7 +501,7 @@
             pltpu.VMEM((rows, 2 * rows), narrow),
             pltpu.VMEM((rows, 1), wide),
             pltpu.VMEM((rows, 1), wide),
-            pltpu.VMEM((rows, 128), wide),
+            pltpu.VMEM((2, rows, 128), wide),
             pltpu.VMEM((8, rows), wide),
             pltpu.VMEM((4, 8, rows), wide),
             pltpu.VMEM((4, rows, 128), wide),
@@ -495,9 +513,18 @@
             dma((PARTS,)), dma((PARTS,)), dma((4,)), dma((4,)), dma((rounds,)), dma((rounds,)),
         ],
         compiler_params=pltpu.CompilerParams(
-            collective_id=0, has_side_effects=True, vmem_limit_bytes=55 * 1024 * 1024
+            collective_id=0, has_side_effects=True, vmem_limit_bytes=50 * 1024 * 1024
         ),
     )(queries, documents, positives)
+    out = jax.ShapeDtypeStruct((rows, width), wide)
+    query_grad, doc_grad = pl.pallas_call(
+        finish,
+        out_shape=[out, out],
+        in_specs=[vmem] * 4,
+        out_specs=[anywhere, anywhere],
+        scratch_shapes=[pltpu.VMEM((rows, width), wide), dma((9,))],
+        compiler_params=pltpu.CompilerParams(vmem_limit_bytes=16 * 1024 * 1024),
+    )(query_grad, doc_dir, own, coefs)
     return query_grad, doc_grad, loss.reshape(())
 
 

time: 121 us -> 119 us (0.983)
  local copies, waits for them, and re-layouts: 4.03 us -> 0 us
    unnamed x2 -> x0, local copies, waits for them, and re-layouts: 4.03 us -> none
    pallas_call x0 -> x1, Pallas kernels: none -> 3.36 us  [on_device_relay(): pl.pallas_call(finish, out_shape=[out, out], in_specs=[vmem] * 4, out_spe...]
    pallas_call x1, Pallas kernels: 115 us -> 113 us  [on_device_relay(): pl.pallas_call(functools.partial(kernel, n_blk, n_grp), out_shape=[grad,...]
where the time goes in v2:
time: 119 us
  Pallas kernels  116 us (97%)
  between operations  2.4 us (2%)
    pallas_call x1, Pallas kernels, on_device_relay(): pl.pallas_call(functools.partial(kernel, n_blk, n_grp), out_shape=[grad,...  113 us
    pallas_call x1, Pallas kernels, on_device_relay(): pl.pallas_call(finish, out_shape=[out, out], in_specs=[vmem] * 4, out_spe...  3.36 us

profile of v2, /device:TPU:0, one launch (start us, length us, event | category | flops | bytes accessed | tf_op | source)
XLA Modules:
  0.0 118.6 jit_solution(10328315587782661004)
XLA Ops:
  0.6 112.8 %shard_map.58 = (f32[256,4096]{1,0:T(8,128)S(1)}, f32[256,4096]{1,0:T(8,128)S(1)}, bf16[512,4096]{1,0:T(8,128)(2,1)S(1)}, f32[2,256,128]{2,1,0:T(8,128)S(1)}, f32[1,1]{1,0:T(1,128)}) custom-call(bf16[256,4096]{1,0:T(8,128)(2,1)} %queries.1, bf16[256,4096]{1,0:T(8,128)(2,1)} %documents.1, s32[1,256]{1,0:T(1,128)} %positives.1), custom_call_target="tpu_custom_call" | custom-call | tf_op jit(solution)/shard_map/pallas_call | solution.py:481
  113.4 3.4 %shard_map.59 = (f32[256,4096]{1,0:T(8,128)}, f32[256,4096]{1,0:T(8,128)}) custom-call(f32[256,4096]{1,0:T(8,128)S(1)} %get-tuple-element.10.query_grad, f32[256,4096]{1,0:T(8,128)S(1)} %get-tuple-element.11.doc_dir, bf16[512,4096]{1,0:T(8,128)(2,1)S(1)} %get-tuple-element.12.own, f32[2,256,128]{2,1,0:T(8,128)S(1)} %get-tuple-element.13.coefs), custom_call_target="tpu_custom_call" | custom-call | tf_op jit(solution)/shard_map/pallas_call | solution.py:520

commit v3 on v2

--- a/solution.py
+++ b/solution.py
@@ -82,8 +82,8 @@
 BUDGET = 3.5
 GROUPS = (10, 4, 2)
 AHEAD = 2
-TILE = 512
-DEEP = 1024
+TILE = 1024
+DEEP = 2048
 NEAR, DIAG, RELAY, SIBLING = range(4)
 
 

time: 119 us -> 116 us (0.975)
  Pallas kernels: 116 us -> 113 us
    pallas_call x1, Pallas kernels: 113 us -> 110 us  [on_device_relay(): pl.pallas_call(functools.partial(kernel, n_blk, n_grp), out_shape=[grad,...]
where the time goes in v3:
time: 116 us
  Pallas kernels  113 us (97%)
  between operations  2.4 us (2%)
    pallas_call x1, Pallas kernels, on_device_relay(): pl.pallas_call(functools.partial(kernel, n_blk, n_grp), out_shape=[grad,...  110 us
    pallas_call x1, Pallas kernels, on_device_relay(): pl.pallas_call(finish, out_shape=[out, out], in_specs=[vmem] * 4, out_spe...  3.36 us

profile of v3, /device:TPU:0, one launch (start us, length us, event | category | flops | bytes accessed | tf_op | source)
XLA Modules:
  0.0 115.8 jit_solution(9931334001238555817)
XLA Ops:
  0.6 110.0 %shard_map.58 = (f32[256,4096]{1,0:T(8,128)S(1)}, f32[256,4096]{1,0:T(8,128)S(1)}, bf16[512,4096]{1,0:T(8,128)(2,1)S(1)}, f32[2,256,128]{2,1,0:T(8,128)S(1)}, f32[1,1]{1,0:T(1,128)}) custom-call(bf16[256,4096]{1,0:T(8,128)(2,1)} %queries.1, bf16[256,4096]{1,0:T(8,128)(2,1)} %documents.1, s32[1,256]{1,0:T(1,128)} %positives.1), custom_call_target="tpu_custom_call" | custom-call | tf_op jit(solution)/shard_map/pallas_call | solution.py:481
  110.6 3.4 %shard_map.59 = (f32[256,4096]{1,0:T(8,128)}, f32[256,4096]{1,0:T(8,128)}) custom-call(f32[256,4096]{1,0:T(8,128)S(1)} %get-tuple-element.10.query_grad, f32[256,4096]{1,0:T(8,128)S(1)} %get-tuple-element.11.doc_dir, bf16[512,4096]{1,0:T(8,128)(2,1)S(1)} %get-tuple-element.12.own, f32[2,256,128]{2,1,0:T(8,128)S(1)} %get-tuple-element.13.coefs), custom_call_target="tpu_custom_call" | custom-call | tf_op jit(solution)/shard_map/pallas_call | solution.py:520
